TPU v7x, 32 devices: a whole 2x2x4 slice. The times are simulated.
32 devices in a mesh: dp: 8 (over z, x), mp: 4 (over y, core).
Axes of the slice: x: 2, y: 2, z: 4, core: 2. Of those that a mesh axis runs over, the one named last changes fastest.
Arguments:
- hidden_in: bfloat16 [8192, 2048], P('dp', 'mp'), may hold values from -6 to 6
- token_ids: int32 [8192], P('dp'), may hold values from 0 to 128001, as said below
- passage_counts: int32 [16], P('dp'), may hold values from 1 to 4, as said below
- positive_doc: int32 [1024], P('dp'), may hold values from 0 to 15
- queries: bfloat16 [1024, 2048], P('dp', 'mp'), may hold values from -6 to 6
- norm_gain: float32 [2048], replicated, may hold values from 0.5 to 1.5
- w_gate: bfloat16 [2048, 7168], P(None, 'mp'), may hold values from -0.125 to 0.125
- w_up: bfloat16 [2048, 7168], P(None, 'mp'), may hold values from -0.125 to 0.125
- w_down: bfloat16 [7168, 2048], P('mp'), may hold values from -0.0625 to 0.0625
Outputs:
- query_loss: float32 [1024], P('dp')
- hidden_grad: bfloat16 [8192, 2048], P('dp', 'mp')
Inputs may be any that keep to these rules, and one draw needn't show every extreme that they name: `passage_counts`: A document has 1 to 4 passages; every draw has a dp index whose documents all have 4. The live passages hold 40 passages in all. `token_ids`: 128001 marks padding; it stands only at the tail of a document's last live passage, and every live passage has a token that is not padding.
All inputs are finite; a program needn't handle non-finite values.
Results may differ from a plain program's by a relative error of at most 0.023.
Values may be sent and summed in bfloat16 or wider, within the bound.
A program may use at most 128 MiB of HBM per device.

v0:
```python
import jax
import jax.numpy as jnp
from jax import lax
from jax.sharding import PartitionSpec as P

L = 128
pad_token = 128001
score_scale = 20.0
loss_seed = 4096.0
norm_epsilon = 1e-05
unit_epsilon = 1e-06


def contract_rows(left, right):
    return lax.dot_general(
        left, right, (((1,), (1,)), ((), ())), preferred_element_type=jnp.float32
    )


def packing_order(received_flag, received_mask, slot_capacity):
    flag = received_flag.reshape(-1).astype(jnp.float32)
    place = jnp.cumsum(flag) - flag
    packed_rows = flag[None, :] * (
        place[None, :] == jnp.arange(slot_capacity, dtype=jnp.float32)[:, None]
    ).astype(jnp.float32)
    packed_half_rows = packed_rows.astype(jnp.bfloat16)
    task_row_mask = jnp.dot(
        packed_half_rows,
        received_mask.reshape(flag.shape[0], -1),
        preferred_element_type=jnp.float32,
    )
    return (packed_rows, packed_half_rows, task_row_mask)


def per_device(
    hidden_in, token_ids, passage_counts, positive_doc, queries, norm_gain, w_gate, w_up, w_down
):
    dp_count = lax.axis_size("dp")
    row_count, part_width = hidden_in.shape
    model_width = norm_gain.shape[0]
    docs_here = passage_counts.shape[0]
    quarters = 4
    block_len = L // quarters
    src_blocks = row_count // block_len
    most_pass = src_blocks // (docs_here * quarters)
    slot_count = src_blocks // dp_count
    slot_capacity = docs_here * 2 * (most_pass + 1)
    passes_here = docs_here * most_pass
    received = dp_count * slot_count
    all_counts = lax.all_gather(passage_counts, "dp", axis=0, tiled=True)
    doc_total = all_counts.shape[0]
    before = (jnp.arange(doc_total, dtype=jnp.int32) < lax.axis_index("dp") * docs_here).astype(
        jnp.int32
    )
    offset = quarters * jnp.sum(all_counts * before)
    block_index = jnp.arange(src_blocks, dtype=jnp.int32)
    live_block = block_index // quarters % most_pass < jnp.repeat(
        passage_counts, most_pass * quarters
    )
    live_int = live_block.astype(jnp.int32)
    global_order = offset + jnp.cumsum(live_int) - live_int
    target = global_order % dp_count
    token_live = (token_ids.reshape(src_blocks, block_len) != pad_token) & live_block[:, None]
    device_hit = live_block.astype(jnp.float32)[:, None] * (
        target[:, None] == jnp.arange(dp_count, dtype=jnp.int32)[None, :]
    ).astype(jnp.float32)
    earlier = jnp.cumsum(device_hit, axis=0) - device_hit
    slot_match = (
        earlier[:, :, None] == jnp.arange(slot_count, dtype=jnp.float32)[None, None, :]
    ).astype(jnp.float32)
    select = (device_hit[:, :, None] * slot_match).reshape(src_blocks, received).T
    select_half = select.astype(jnp.bfloat16)
    send_mask = jnp.dot(
        select_half, token_live.astype(jnp.bfloat16), preferred_element_type=jnp.float32
    )
    send_mask = send_mask.astype(jnp.bfloat16).reshape(dp_count, slot_count, block_len)
    send_flag = jnp.sum(select, axis=1).astype(jnp.bfloat16).reshape(dp_count, slot_count)
    mp_start = lax.axis_index("mp") * part_width
    send = jnp.dot(
        select_half,
        hidden_in.reshape(src_blocks, block_len * part_width),
        preferred_element_type=jnp.float32,
    )
    send = send.astype(jnp.bfloat16).reshape(dp_count, slot_count, block_len, part_width)
    got, received_mask, received_flag = (
        lax.all_to_all(send, "dp", split_axis=0, concat_axis=0, tiled=True),
        lax.all_to_all(send_mask, "dp", split_axis=0, concat_axis=0, tiled=True),
        lax.all_to_all(send_flag, "dp", split_axis=0, concat_axis=0, tiled=True),
    )
    packed_rows, packed_half_rows, task_row_mask = packing_order(
        received_flag, received_mask, slot_capacity
    )
    own_rows = jnp.dot(
        packed_half_rows,
        got.reshape(received, block_len * part_width),
        preferred_element_type=jnp.float32,
    )
    own_rows = own_rows.astype(jnp.bfloat16).reshape(slot_capacity * block_len, part_width)
    task_rows = lax.all_gather(own_rows, "mp", axis=1, tiled=True)
    row_float = task_rows.astype(jnp.float32)
    rms_scale = lax.rsqrt(jnp.mean(row_float * row_float, axis=1, keepdims=True) + norm_epsilon)
    normed = (row_float * rms_scale * norm_gain[None, :]).astype(jnp.bfloat16)
    gate = jnp.dot(normed, w_gate, preferred_element_type=jnp.float32)
    up = jnp.dot(normed, w_up, preferred_element_type=jnp.float32)
    sigmoid_gate = jax.nn.sigmoid(gate)
    hidden = (gate * sigmoid_gate * up).astype(jnp.bfloat16)
    layer_part = jnp.dot(hidden, w_down, preferred_element_type=jnp.float32)
    token_weight = task_row_mask[:, :, None]
    layer_pool = jnp.sum(
        layer_part.reshape(slot_capacity, block_len, model_width) * token_weight, axis=1
    )
    layer_pool = lax.psum_scatter(
        layer_pool.astype(jnp.bfloat16), "mp", scatter_dimension=1, tiled=True
    ).astype(jnp.float32)
    own_input = own_rows.astype(jnp.float32)
    pooled = (
        jnp.sum(own_input.reshape(slot_capacity, block_len, part_width) * token_weight, axis=1)
        + layer_pool
    )
    spread = jnp.dot(packed_rows.T, pooled, precision=lax.Precision.HIGHEST)
    home = lax.all_to_all(
        spread.reshape(dp_count, slot_count, part_width).astype(jnp.bfloat16),
        "dp",
        split_axis=0,
        concat_axis=0,
        tiled=True,
    ).astype(jnp.float32)
    block_sums = jnp.dot(
        select.T, home.reshape(received, part_width), precision=lax.Precision.HIGHEST
    )
    passage_sum = block_sums.reshape(passes_here, quarters, part_width).sum(axis=1)
    token_total = jnp.sum(
        token_live.reshape(passes_here, quarters * block_len).astype(jnp.float32), axis=1
    )
    divisor = jnp.maximum(token_total, 1.0)
    passage_vec = (passage_sum / divisor[:, None]).astype(jnp.bfloat16)
    all_vec = lax.all_gather(passage_vec, "dp", axis=0, tiled=True)
    pass_total = all_vec.shape[0]
    all_live = (
        jnp.arange(pass_total, dtype=jnp.int32) % most_pass < jnp.repeat(all_counts, most_pass)
    ).astype(jnp.float32)
    vec_float = all_vec.astype(jnp.float32)
    query_float = queries.astype(jnp.float32)
    score_part = contract_rows(queries, all_vec)
    raw_score, passage_sq, query_sq = (
        lax.psum(score_part.astype(jnp.bfloat16), "mp").astype(jnp.float32),
        lax.psum(jnp.sum(vec_float * vec_float, axis=1).astype(jnp.bfloat16), "mp").astype(
            jnp.float32
        ),
        lax.psum(jnp.sum(query_float * query_float, axis=1).astype(jnp.bfloat16), "mp").astype(
            jnp.float32
        ),
    )
    query_scale = lax.rsqrt(query_sq + unit_epsilon)
    passage_scale = lax.rsqrt(passage_sq + unit_epsilon)
    scores = score_scale * raw_score * query_scale[:, None] * passage_scale[None, :]
    weights = all_live[None, :] * jnp.exp(scores)
    doc_mass = weights.reshape(queries.shape[0], doc_total, most_pass).sum(axis=2)
    total_mass = doc_mass.sum(axis=1)
    positive_hit = (
        positive_doc[:, None] == jnp.arange(doc_total, dtype=jnp.int32)[None, :]
    ).astype(jnp.float32)
    positive_mass = jnp.sum(doc_mass * positive_hit, axis=1)
    query_loss = jnp.log(total_mass) - jnp.log(positive_mass)
    positive_pass = jnp.repeat(positive_hit, most_pass, axis=1)
    coefficient = (
        loss_seed
        * score_scale
        * query_scale[:, None]
        * (weights / total_mass[:, None] - positive_pass * weights / positive_mass[:, None])
    )
    weighted_queries = lax.dot_general(
        coefficient.astype(jnp.bfloat16),
        queries,
        (((0,), (0,)), ((), ())),
        preferred_element_type=jnp.float32,
    )
    norm_term = jnp.sum(coefficient * raw_score, axis=0)
    vec_grad, norm_grad = (
        lax.psum_scatter(
            weighted_queries.astype(jnp.bfloat16), "dp", scatter_dimension=0, tiled=True
        ).astype(jnp.float32),
        lax.psum_scatter(
            norm_term.astype(jnp.bfloat16), "dp", scatter_dimension=0, tiled=True
        ).astype(jnp.float32),
    )
    own_scale = lax.dynamic_slice_in_dim(
        passage_scale, lax.axis_index("dp") * passes_here, passes_here
    )
    own_vec = passage_vec.astype(jnp.float32)
    vec_change = own_scale[:, None] * vec_grad - own_vec * (own_scale**3 * norm_grad)[:, None]
    token_grad = (vec_change / divisor[:, None]).astype(jnp.bfloat16)
    block_grad = jnp.repeat(token_grad, quarters, axis=0)
    grad_send = jnp.dot(select_half, block_grad, preferred_element_type=jnp.float32).astype(
        jnp.bfloat16
    )
    grad_got = lax.all_to_all(
        grad_send.reshape(dp_count, slot_count, part_width),
        "dp",
        split_axis=0,
        concat_axis=0,
        tiled=True,
    )
    grad_task = jnp.dot(
        packed_half_rows, grad_got.reshape(received, part_width), preferred_element_type=jnp.float32
    ).astype(jnp.bfloat16)
    grad_full = lax.all_gather(grad_task, "mp", axis=1, tiled=True)
    out_grad = (
        (token_weight * grad_full[:, None, :].astype(jnp.float32))
        .astype(jnp.bfloat16)
        .reshape(slot_capacity * block_len, model_width)
    )
    own_out_grad = (token_weight * grad_task[:, None, :].astype(jnp.float32)).reshape(
        slot_capacity * block_len, part_width
    )
    hidden_grad = contract_rows(out_grad, w_down)
    gate_grad = (hidden_grad * up * sigmoid_gate * (1.0 + gate * (1.0 - sigmoid_gate))).astype(
        jnp.bfloat16
    )
    up_grad = (hidden_grad * gate * sigmoid_gate).astype(jnp.bfloat16)
    normed_grad = contract_rows(gate_grad, w_gate) + contract_rows(up_grad, w_up)
    own_gain = lax.dynamic_slice_in_dim(norm_gain, mp_start, part_width)
    normed_full = lax.psum(normed_grad.astype(jnp.bfloat16), "mp").astype(jnp.float32)
    inner = jnp.mean(row_float * norm_gain[None, :] * normed_full, axis=1)
    own_normed = lax.dynamic_slice_in_dim(normed_full, mp_start, part_width, 1)
    input_grad = (
        own_out_grad
        + rms_scale * own_gain[None, :] * own_normed
        - own_input * rms_scale**3 * inner[:, None]
    )
    input_half = input_grad.astype(jnp.bfloat16).reshape(slot_capacity, block_len * part_width)
    back = jnp.dot(packed_half_rows.T, input_half, preferred_element_type=jnp.float32).astype(
        jnp.bfloat16
    )
    back_got = lax.all_to_all(
        back.reshape(dp_count, slot_count, block_len * part_width),
        "dp",
        split_axis=0,
        concat_axis=0,
        tiled=True,
    )
    grad_rows = jnp.dot(
        select_half.T,
        back_got.reshape(received, block_len * part_width),
        preferred_element_type=jnp.float32,
    )
    return (query_loss, grad_rows.astype(jnp.bfloat16).reshape(row_count, part_width))


def solution(mesh):
    return jax.shard_map(
        per_device,
        mesh=mesh,
        in_specs=(
            P("dp", "mp"),
            P("dp"),
            P("dp"),
            P("dp"),
            P("dp", "mp"),
            P(),
            P(None, "mp"),
            P(None, "mp"),
            P("mp", None),
        ),
        out_specs=(P("dp"), P("dp", "mp")),
        check_vma=False,
    )
```

profile of v0, /device:TPU:0, one launch (start us, length us, event | category | flops | bytes accessed | tf_op | source)
XLA Modules:
  0.0 407.2 jit_solution(3093660262261133668)
XLA Ops:
  11.1 13.1 %all-reduce = s32[16]{0:T(128)S(1)} all-reduce(s32[16]{0:T(128)S(1)} %dynamic-update-slice), channel_id=1, replica_groups=mesh['dp'=8,'mp'=4] {'dp'}, use_global_device_ids=true, to_apply=%add | all-reduce | flops 16 | bytes 128
  26.8 3.3 all-to-all-start
  33.7 3.0 all-to-all-done
  36.6 3.7 all-to-all-start.1
  40.7 21.8 %all-to-all-done.1 = bf16[8,4,32,512]{3,2,1,0:T(8,128)(2,1)S(1)} async-done(((bf16[8,4,32,512]{3,2,1,0:T(8,128)(2,1)}), bf16[8,4,32,512]{3,2,1,0:T(8,128)(2,1)S(1)}, u32[]{:S(2)}, u32[]{:S(2)}) %all-to-all-start.1) | async-done | bytes 1048608 | tf_op jit(solution)/shard_map/all_to_all | solution.py:86
  65.8 3.4 all-to-all-start.2
  70.1 5.6 %all-to-all-done.2 = bf16[8,4,32]{2,1,0:T(4,128)(2,1)S(1)} async-done(((bf16[8,4,32]{2,1,0:T(4,128)(2,1)}), bf16[8,4,32]{2,1,0:T(4,128)(2,1)S(1)}, u32[]{:S(2)}, u32[]{:S(2)}) %all-to-all-start.2) | async-done | bytes 2080 | tf_op jit(solution)/shard_map/all_to_all | solution.py:87
  75.8 2.1 copy.62
  77.9 11.5 %all-gather.2.cloned.1.call-done = bf16[640,2048]{1,0:T(8,128)(2,1)} async-done(((bf16[640,512]{1,0:T(8,128)(2,1)}), bf16[640,2048]{1,0:T(8,128)(2,1)}) %all-gather.2.cloned.1.call-update) | async-done | bytes 2621456 | tf_op jit(solution)/shard_map/all_gather | solution.py:99
  89.4 2.5 fusion
  92.0 9.0 %fusion.15 = f32[640,1792]{1,0:T(8,128)S(1)} fusion(bf16[2048,1792]{1,0:T(8,128)(2,1)} %param.16, bf16[640,2048]{1,0:T(8,128)(2,1)} %all-gather.2.cloned.1.call-done, f32[2048]{0:T(1024)S(1)} %copy-done.4, f32[640]{0:T(1024)S(1)} %get-tuple-element.14), kind=kOutput, calls=%fused_computation.38 | convolution fusion | flops 4702863360 | bytes 14559744 | tf_op jit(solution)/shard_map/dot_general | solution.py:104
  101.0 5.0 %fusion.17 = f32[640,1792]{1,0:T(8,128)S(1)} fusion(bf16[2048,1792]{1,0:T(8,128)(2,1)S(1)} %bitcast.76, bf16[640,2048]{1,0:T(8,128)(2,1)S(1)} %copy-done, f32[2048]{0:T(1024)S(1)} %copy-done.4, f32[640]{0:T(1024)S(1)} %get-tuple-element.14), kind=kOutput, calls=%fused_computation.39 | convolution fusion | flops 4702863360 | bytes 14559744 | tf_op jit(solution)/shard_map/dot_general | solution.py:103
  106.0 5.0 %fusion.6 = f32[640,2048]{1,0:T(8,128)S(1)} fusion(bf16[1792,2048]{1,0:T(8,128)(2,1)S(1)} %bitcast.74, f32[640,1792]{1,0:T(8,128)S(1)} %fusion.15, f32[640,1792]{1,0:T(8,128)S(1)} %fusion.17), kind=kOutput, calls=%fused_computation.20 | convolution fusion | flops 4704501760 | bytes 21757952 | tf_op jit(solution)/shard_map/dot_general | solution.py:107
  111.1 1.6 multiply_reduce_fusion
  112.7 1.6 fusion.10
  114.3 18.1 %reduce-scatter.3.cloned.1.call-done = bf16[20,512]{1,0:T(8,128)(2,1)} async-done(((bf16[20,2048]{1,0:T(8,128)(2,1)}), bf16[20,512]{1,0:T(8,128)(2,1)}) %reduce-scatter.3.cloned.1.call-update) | async-done | bytes 20496 | tf_op jit(solution)/shard_map/reduce_scatter | solution.py:112
  134.0 5.5 %all-to-all-start.3 = ((bf16[8,4,512]{2,1,0:T(4,128)(2,1)}), bf16[8,4,512]{2,1,0:T(4,128)(2,1)S(1)}, u32[]{:S(2)}, u32[]{:S(2)}) async-start(bf16[8,4,512]{2,1,0:T(4,128)(2,1)} %convert_element_type.242), calls=%async_computation.4 | async-start | bytes 65536 | tf_op jit(solution)/shard_map/all_to_all | solution.py:121
  140.6 5.6 %all-to-all-done.3 = bf16[8,4,512]{2,1,0:T(4,128)(2,1)S(1)} async-done(((bf16[8,4,512]{2,1,0:T(4,128)(2,1)}), bf16[8,4,512]{2,1,0:T(4,128)(2,1)S(1)}, u32[]{:S(2)}, u32[]{:S(2)}) %all-to-all-start.3) | async-done | bytes 32800 | tf_op jit(solution)/shard_map/all_to_all | solution.py:121
  146.5 30.6 %all_gather.14 = bf16[64,512]{1,0:T(8,128)(2,1)S(1)} all-gather(bf16[8,512]{1,0:T(8,128)(2,1)S(1)} %divide_convert_fusion.1), channel_id=1, replica_groups=mesh['dp'=8,'mp'=4] {'dp'}, dimensions={0}, use_global_device_ids=true | all-gather | bytes 73728 | tf_op jit(solution)/shard_map/all_gather | solution.py:137
  177.3 10.4 %all-reduce.2 = (bf16[128,64]{0,1:T(8,128)(2,1)S(1)}, bf16[64]{0:T(256)(128)(2,1)S(1)}, bf16[128]{0:T(256)(128)(2,1)S(1)}) all-reduce(bf16[128,64]{0,1:T(8,128)(2,1)S(1)} %fusion.14, bf16[64]{0:T(256)(128)(2,1)S(1)} %multiply_reduce_fusion.2, bf16[128]{0:T(256)(128)(2,1)S(1)} %multiply_reduce_fusion.1), channel_id=1, replica_groups=mesh['dp'=8,'mp'=4] {'mp'}, use_global_device_ids=true, to_apply=%region_11.12 | all-reduce | flops 8384 | bytes 33536 | tf_op jit(solution)/shard_map/psum | solution.py:146
  188.9 17.8 %all-reduce.1 = bf16[64]{0:T(256)(128)(2,1)S(1)} all-reduce(bf16[64]{0:T(256)(128)(2,1)S(1)} %fusion.24), channel_id=4, replica_groups=mesh['dp'=8,'mp'=4] {'dp'}, use_global_device_ids=true, to_apply=%region_21.22.clone | all-reduce | flops 64 | bytes 256
  206.8 40.9 %reduce-scatter.5.cloned.1.call-done = bf16[8,512]{1,0:T(8,128)(2,1)} async-done(((bf16[64,512]{1,0:T(8,128)(2,1)}), bf16[8,512]{1,0:T(8,128)(2,1)}) %reduce-scatter.5.cloned.1.call-update) | async-done | bytes 8208 | tf_op jit(solution)/shard_map/reduce_scatter | solution.py:180
  249.3 3.6 all-to-all-start.4
  253.1 6.6 %all-to-all-done.4 = bf16[8,4,512]{2,1,0:T(4,128)(2,1)S(1)} async-done(((bf16[8,4,512]{2,1,0:T(4,128)(2,1)}), bf16[8,4,512]{2,1,0:T(4,128)(2,1)S(1)}, u32[]{:S(2)}, u32[]{:S(2)}) %all-to-all-start.4) | async-done | bytes 32800 | tf_op jit(solution)/shard_map/all_to_all | solution.py:197
  259.8 5.5 %all_gather.15 = bf16[20,2048]{1,0:T(8,128)(2,1)S(1)} all-gather(bf16[20,512]{1,0:T(8,128)(2,1)S(1)} %get-tuple-element.22), channel_id=1, replica_groups=mesh['dp'=8,'mp'=4] {'mp'}, dimensions={1}, use_global_device_ids=true | all-gather | bytes 102400 | tf_op jit(solution)/shard_map/all_gather | solution.py:207
  265.7 9.9 %fusion.72 = f32[640,1792]{1,0:T(8,128)} fusion(bf16[640,2048]{1,0:T(8,128)(2,1)S(1)} %fusion.5, bf16[1792,2048]{1,0:T(8,128)(2,1)} %param.17), kind=kOutput, calls=%fused_computation.149 | convolution fusion | flops 4697620480 | bytes 14548992 | tf_op jit(solution)/shard_map/dot_general | solution.py:15
  275.6 14.2 %fusion.9 = f32[640,2048]{1,0:T(8,128)} fusion(bf16[2048,1792]{1,0:T(8,128)(2,1)S(1)} %bitcast.78, f32[640,1792]{1,0:T(8,128)} %copy-done.8, f32[640,1792]{1,0:T(8,128)} %fusion.72, f32[640,1792]{1,0:T(8,128)} %copy-done.9), kind=kOutput, calls=%fused_computation.23 | convolution fusion | flops 4709089280 | bytes 26345472 | tf_op jit(solution)/shard_map/dot_general | solution.py:15
  289.8 13.7 %add_convert_fusion = bf16[640,2048]{1,0:T(8,128)(2,1)} fusion(f32[640,2048]{1,0:T(8,128)} %fusion.9, bf16[2048,1792]{1,0:T(8,128)(2,1)} %param.16, f32[640,1792]{1,0:T(8,128)} %fusion.72, f32[640,1792]{1,0:T(8,128)} %copy-done.8), kind=kOutput, calls=%fused_computation.14 | convolution fusion | flops 4707123200 | bytes 24379392 | tf_op jit(solution)/shard_map/dot_general | solution.py:15
  303.6 57.3 %all-reduce.5.cloned.1.call-done = bf16[640,2048]{1,0:T(8,128)(2,1)} async-done(((bf16[640,2048]{1,0:T(8,128)(2,1)}), bf16[640,2048]{1,0:T(8,128)(2,1)}) %all-reduce.5.cloned.1.call-update) | async-done | bytes 2621456 | tf_op jit(solution)/shard_map/psum | solution.py:223
  361.0 2.8 fusion.4
  367.4 5.5 %all-to-all-start.5 = ((bf16[8,4,16384]{2,1,0:T(4,128)(2,1)}), bf16[8,4,16384]{2,1,0:T(4,128)(2,1)S(1)}, u32[]{:S(2)}, u32[]{:S(2)}) async-start(bf16[8,4,16384]{2,1,0:T(4,128)(2,1)} %reshape.491), calls=%async_computation.7 | async-start | bytes 2097152 | tf_op jit(solution)/shard_map/all_to_all | solution.py:235
  373.5 25.1 %all-to-all-done.5 = bf16[8,4,16384]{2,1,0:T(4,128)(2,1)S(1)} async-done(((bf16[8,4,16384]{2,1,0:T(4,128)(2,1)}), bf16[8,4,16384]{2,1,0:T(4,128)(2,1)S(1)}, u32[]{:S(2)}, u32[]{:S(2)}) %all-to-all-start.5) | async-done | bytes 1048608 | tf_op jit(solution)/shard_map/all_to_all | solution.py:235
  (137 shorter events, 25.6 us)
Async XLA Ops:
  26.8 9.8 %all-to-all-start = ((bf16[8,1,4]{2,1,0:T(2,128)(2,1)}), bf16[8,1,4]{2,1,0:T(2,128)(2,1)S(1)}, u32[]{:S(2)}, u32[]{:S(2)}) async-start(bf16[8,1,4]{2,1,0:T(2,128)(2,1)} %copy.53), calls=%async_computation | async-start | bytes 8192 | tf_op jit(solution)/shard_map/all_to_all | solution.py:88
  36.6 28.3 %copy-start.5 = (s32[1024]{0:T(1024)S(1)}, s32[1024]{0:T(1024)}, u32[]{:S(2)}) copy-start(s32[1024]{0:T(1024)} %param.10) | copy-start | bytes 12292
  36.6 32.9 %copy-start.7 = (s32[2]{0:T(128)S(1)}, s32[2]{0:T(128)}, u32[]{:S(2)}) copy-start(s32[2]{0:T(128)} %param.11) | copy-start | bytes 28
  36.6 33.5 %copy-start.6 = (s32[128]{0:T(128)S(1)}, s32[128]{0:T(128)}, u32[]{:S(2)}) copy-start(s32[128]{0:T(128)} %param.12) | copy-start | bytes 1540
  36.6 25.9 %all-to-all-start.1 = ((bf16[8,4,32,512]{3,2,1,0:T(8,128)(2,1)}), bf16[8,4,32,512]{3,2,1,0:T(8,128)(2,1)S(1)}, u32[]{:S(2)}, u32[]{:S(2)}) async-start(bf16[8,4,32,512]{3,2,1,0:T(8,128)(2,1)} %bitcast.17), calls=%async_computation.1 | async-start | bytes 2097152 | tf_op jit(solution)/shard_map/all_to_all | solution.py:86
  40.3 49.1 %all-gather.2.cloned.1.call-start = ((), (), s32[]{:S(2)}) async-start(), calls=%async_computation.8 | async-start | bytes 3276800 | tf_op jit(solution)/shard_map/all_gather | solution.py:99
  63.6 28.4 %copy-start.4 = (f32[2048]{0:T(1024)S(1)}, f32[2048]{0:T(1024)}, u32[]{:S(2)}) copy-start(f32[2048]{0:T(1024)} %param.14) | copy-start | bytes 24580
  65.8 9.9 %all-to-all-start.2 = ((bf16[8,4,32]{2,1,0:T(4,128)(2,1)}), bf16[8,4,32]{2,1,0:T(4,128)(2,1)S(1)}, u32[]{:S(2)}, u32[]{:S(2)}) async-start(bf16[8,4,32]{2,1,0:T(4,128)(2,1)} %bitcast.4), calls=%async_computation.2 | async-start | bytes 16384 | tf_op jit(solution)/shard_map/all_to_all | solution.py:87
  69.2 63.2 %reduce-scatter.3.cloned.1.call-start = ((), (), s32[]{:S(2)}) async-start(), calls=%async_computation.9 | async-start | bytes 122880 | tf_op jit(solution)/shard_map/reduce_scatter | solution.py:112
  89.4 11.5 %slice-start.2 = ((s8[7340032]{0:T(1024)(128)(4,1)}), s8[4194304]{0:T(1024)(128)(4,1)S(1)}, s32[]{:S(2)}) async-start(s8[7340032]{0:T(1024)(128)(4,1)} %bitcast.75), calls=%async_computation.14 | async-start | bytes 8388608
  91.9 9.0 %copy-start = (bf16[640,2048]{1,0:T(8,128)(2,1)S(1)}, bf16[640,2048]{1,0:T(8,128)(2,1)}, u32[]{:S(2)}) copy-start(bf16[640,2048]{1,0:T(8,128)(2,1)} %all-gather.2.cloned.1.call-done) | copy-start | bytes 7864324
  91.9 9.0 %slice-start.3 = ((s8[7340032]{0:T(1024)(128)(4,1)}), s8[3145728]{0:T(1024)(128)(4,1)S(1)}, s32[]{:S(2)}) async-start(s8[7340032]{0:T(1024)(128)(4,1)} %bitcast.75), calls=%async_computation.15 | async-start | bytes 6291456
  91.9 14.1 %slice-start = ((s8[7340032]{0:T(1024)(128)(4,1)}), s8[4194304]{0:T(1024)(128)(4,1)S(1)}, s32[]{:S(2)}) async-start(s8[7340032]{0:T(1024)(128)(4,1)} %bitcast.73), calls=%async_computation.12 | async-start | bytes 8388608
  101.0 5.0 %copy-start.9 = (f32[640,1792]{1,0:T(8,128)}, f32[640,1792]{1,0:T(8,128)S(1)}, u32[]{:S(2)}) copy-start(f32[640,1792]{1,0:T(8,128)S(1)} %fusion.15) | copy-start | bytes 13762564
  101.0 5.0 %slice-start.1 = ((s8[7340032]{0:T(1024)(128)(4,1)}), s8[3145728]{0:T(1024)(128)(4,1)S(1)}, s32[]{:S(2)}) async-start(s8[7340032]{0:T(1024)(128)(4,1)} %bitcast.73), calls=%async_computation.13 | async-start | bytes 6291456
  106.0 5.0 %copy-start.8 = (f32[640,1792]{1,0:T(8,128)}, f32[640,1792]{1,0:T(8,128)S(1)}, u32[]{:S(2)}) copy-start(f32[640,1792]{1,0:T(8,128)S(1)} %fusion.17) | copy-start | bytes 13762564
  111.0 28.5 %copy-start.3 = (bf16[128,512]{1,0:T(8,128)(2,1)S(1)}, bf16[128,512]{1,0:T(8,128)(2,1)}, u32[]{:S(2)}) copy-start(bf16[128,512]{1,0:T(8,128)(2,1)} %param.13) | copy-start | bytes 393220
  134.0 12.2 %all-to-all-start.3 = ((bf16[8,4,512]{2,1,0:T(4,128)(2,1)}), bf16[8,4,512]{2,1,0:T(4,128)(2,1)S(1)}, u32[]{:S(2)}, u32[]{:S(2)}) async-start(bf16[8,4,512]{2,1,0:T(4,128)(2,1)} %convert_element_type.242), calls=%async_computation.4 | async-start | bytes 65536 | tf_op jit(solution)/shard_map/all_to_all | solution.py:121
  139.5 108.2 %reduce-scatter.5.cloned.1.call-start = ((), (), s32[]{:S(2)}) async-start(), calls=%async_computation.10 | async-start | bytes 73728 | tf_op jit(solution)/shard_map/reduce_scatter | solution.py:180
  249.3 10.3 %all-to-all-start.4 = ((bf16[8,4,512]{2,1,0:T(4,128)(2,1)}), bf16[8,4,512]{2,1,0:T(4,128)(2,1)S(1)}, u32[]{:S(2)}, u32[]{:S(2)}) async-start(bf16[8,4,512]{2,1,0:T(4,128)(2,1)} %reshape.488), calls=%async_computation.6 | async-start | bytes 65536 | tf_op jit(solution)/shard_map/all_to_all | solution.py:197
  253.0 108.0 %all-reduce.5.cloned.1.call-start = ((), (), s32[]{:S(2)}) async-start(), calls=%async_computation.11 | async-start | bytes 5242880 | tf_op jit(solution)/shard_map/psum | solution.py:223
  265.4 10.2 %slice-start.4 = ((s8[7340032]{0:T(1024)(128)(4,1)}), s8[4194304]{0:T(1024)(128)(4,1)S(1)}, s32[]{:S(2)}) async-start(s8[7340032]{0:T(1024)(128)(4,1)} %bitcast.77), calls=%async_computation.16 | async-start | bytes 8388608
  265.7 9.9 %slice-start.5 = ((s8[7340032]{0:T(1024)(128)(4,1)}), s8[3145728]{0:T(1024)(128)(4,1)S(1)}, s32[]{:S(2)}) async-start(s8[7340032]{0:T(1024)(128)(4,1)} %bitcast.77), calls=%async_computation.17 | async-start | bytes 6291456
  361.0 2.9 copy-start.1
  363.8 1.1 copy-start.2
  367.4 31.1 %all-to-all-start.5 = ((bf16[8,4,16384]{2,1,0:T(4,128)(2,1)}), bf16[8,4,16384]{2,1,0:T(4,128)(2,1)S(1)}, u32[]{:S(2)}, u32[]{:S(2)}) async-start(bf16[8,4,16384]{2,1,0:T(4,128)(2,1)} %reshape.491), calls=%async_computation.7 | async-start | bytes 2097152 | tf_op jit(solution)/shard_map/all_to_all | solution.py:235
Sparse Core Ops, SparseCore 0:
  65.0 24.3 all-gather.1
  112.8 19.5 reduce-scatter.2
  188.8 58.8 reduce-scatter.4
  303.7 57.2 all-reduce.4
where the time goes:
time: 408 us; the launch traced here: 407 us
  waiting for transfers between devices  196 us (48%)
  blocking collectives  77.4 us (19%)
  matrix products  61.8 us (15%)
  starting transfers between devices  25.4 us (6%)
  local copies, waits for them, and re-layouts  16.9 us (4%)
  between operations  16.3 us (4%)
  other arithmetic  13.7 us (3%)
    psum x1, waiting for transfers between devices, per_device(): lax.psum(normed_grad.astype(jnp.bfloat16), 'mp').astype(jnp.float32)  57.3 us
    reduce_scatter x1, waiting for transfers between devices, per_device(): lax.psum_scatter(weighted_queries.astype(jnp.bfloat16), 'dp', scatter_dim...  40.9 us
    dot_general x4, matrix products, contract_rows(): lax.dot_general(left, right, (((1,), (1,)), ((), ())), preferred_element_...  37.9 us
    unnamed x2, blocking collectives  30.9 us
    all_gather x1, blocking collectives, per_device(): all_vec = lax.all_gather(passage_vec, 'dp', axis=0, tiled=True)  30.6 us
    all_to_all x1, waiting for transfers between devices, per_device(): lax.all_to_all(back.reshape(dp_count, slot_count, block_len * part_width)...  25.1 us
    all_to_all x1, waiting for transfers between devices, per_device(): lax.all_to_all(send, 'dp', split_axis=0, concat_axis=0, tiled=True)  21.8 us
    reduce_scatter x1, waiting for transfers between devices, per_device(): lax.psum_scatter(layer_pool.astype(jnp.bfloat16), 'mp', scatter_dimension...  18.1 us
  transfers between devices with their start and end apart: 10, of which 10 were waited for; matrix products, arithmetic and copies ran while one was open for 3% of the time, Pallas kernels for 0%

commit v1 on v0

--- a/solution.py
+++ b/solution.py
@@ -9,6 +9,11 @@
 loss_seed = 4096.0
 norm_epsilon = 1e-05
 unit_epsilon = 1e-06
+
+
+def gather_and_add(x, mesh_axis):
+    pieces = lax.all_gather(x, mesh_axis)
+    return jnp.sum(pieces, axis=0)
 
 
 def contract_rows(left, right):
@@ -220,7 +225,7 @@
     up_grad = (hidden_grad * gate * sigmoid_gate).astype(jnp.bfloat16)
     normed_grad = contract_rows(gate_grad, w_gate) + contract_rows(up_grad, w_up)
     own_gain = lax.dynamic_slice_in_dim(norm_gain, mp_start, part_width)
-    normed_full = lax.psum(normed_grad.astype(jnp.bfloat16), "mp").astype(jnp.float32)
+    normed_full = gather_and_add(normed_grad.astype(jnp.bfloat16), "mp").astype(jnp.float32)
     inner = jnp.mean(row_float * norm_gain[None, :] * normed_full, axis=1)
     own_normed = lax.dynamic_slice_in_dim(normed_full, mp_start, part_width, 1)
     input_grad = (

time: 408 us -> 426 us (1.044)
  waiting for transfers between devices: 196 us -> 209 us
    all_gather x0 -> x1, waiting for transfers between devices: none -> 67.6 us  [gather_and_add(): pieces = lax.all_gather(x, mesh_axis)]
    psum x1 -> x0, waiting for transfers between devices: 57.3 us -> none  [per_device(): lax.psum(normed_grad.astype(jnp.bfloat16), 'mp').astype(jnp.float32)]
    reduce_sum x0 -> x1, other arithmetic: none -> 7.28 us  [gather_and_add(): return jnp.sum(pieces, axis=0)]
  transfers between devices with their start and end apart: 10 -> 10, of which waited for: 10 -> 10; matrix products, arithmetic and copies ran while one was open for 3% -> 2% of each run, Pallas kernels for 0% -> 0%
where the time goes in v1:
time: 426 us; the launch traced here: 425 us
  waiting for transfers between devices  209 us (49%)
  blocking collectives  77.2 us (18%)
  matrix products  63.1 us (15%)
  starting transfers between devices  25.4 us (6%)
  other arithmetic  17.8 us (4%)
  local copies, waits for them, and re-layouts  16.6 us (4%)
  between operations  16.2 us (4%)
    all_gather x1, waiting for transfers between devices, gather_and_add(): pieces = lax.all_gather(x, mesh_axis)  67.6 us
    reduce_scatter x1, waiting for transfers between devices, per_device(): lax.psum_scatter(weighted_queries.astype(jnp.bfloat16), 'dp', scatter_dim...  41 us
    dot_general x4, matrix products, contract_rows(): lax.dot_general(left, right, (((1,), (1,)), ((), ())), preferred_element_...  38.1 us
    unnamed x2, blocking collectives  30.9 us
    all_gather x1, blocking collectives, per_device(): all_vec = lax.all_gather(passage_vec, 'dp', axis=0, tiled=True)  30.6 us
    all_to_all x1, waiting for transfers between devices, per_device(): lax.all_to_all(back.reshape(dp_count, slot_count, block_len * part_width)...  25.7 us
    all_to_all x1, waiting for transfers between devices, per_device(): lax.all_to_all(send, 'dp', split_axis=0, concat_axis=0, tiled=True)  21.8 us
    reduce_scatter x1, waiting for transfers between devices, per_device(): lax.psum_scatter(layer_pool.astype(jnp.bfloat16), 'mp', scatter_dimension...  19.5 us
  transfers between devices with their start and end apart: 10, of which 10 were waited for; matrix products, arithmetic and copies ran while one was open for 2% of the time, Pallas kernels for 0%

profile of v1, /device:TPU:0, one launch (start us, length us, event | category | flops | bytes accessed | tf_op | source)
XLA Modules:
  0.0 425.2 jit_solution(7612486885559917472)
XLA Ops:
  8.2 1.3 fusion.69
  11.1 13.1 %all-reduce = s32[16]{0:T(128)S(1)} all-reduce(s32[16]{0:T(128)S(1)} %dynamic-update-slice), channel_id=1, replica_groups=mesh['dp'=8,'mp'=4] {'dp'}, use_global_device_ids=true, to_apply=%add | all-reduce | flops 16 | bytes 128
  26.8 3.3 all-to-all-start
  30.3 1.6 reshape.477
  33.7 3.0 all-to-all-done
  36.6 3.7 all-to-all-start.1
  40.7 21.8 %all-to-all-done.1 = bf16[8,4,32,512]{3,2,1,0:T(8,128)(2,1)S(1)} async-done(((bf16[8,4,32,512]{3,2,1,0:T(8,128)(2,1)}), bf16[8,4,32,512]{3,2,1,0:T(8,128)(2,1)S(1)}, u32[]{:S(2)}, u32[]{:S(2)}) %all-to-all-start.1) | async-done | bytes 1048608 | tf_op jit(solution)/shard_map/all_to_all | solution.py:91
  65.8 3.4 all-to-all-start.2
  70.1 5.6 %all-to-all-done.2 = bf16[8,4,32]{2,1,0:T(4,128)(2,1)S(1)} async-done(((bf16[8,4,32]{2,1,0:T(4,128)(2,1)}), bf16[8,4,32]{2,1,0:T(4,128)(2,1)S(1)}, u32[]{:S(2)}, u32[]{:S(2)}) %all-to-all-start.2) | async-done | bytes 2080 | tf_op jit(solution)/shard_map/all_to_all | solution.py:92
  76.8 12.7 %all-gather.4.cloned.1.call-done = bf16[640,2048]{1,0:T(8,128)(2,1)} async-done(((bf16[640,512]{1,0:T(8,128)(2,1)}), bf16[640,2048]{1,0:T(8,128)(2,1)}) %all-gather.4.cloned.1.call-update) | async-done | bytes 2621456 | tf_op jit(solution)/shard_map/all_gather | solution.py:104
  89.4 2.5 fusion
  92.0 10.1 %fusion.15 = f32[640,1792]{1,0:T(8,128)S(1)} fusion(bf16[2048,1792]{1,0:T(8,128)(2,1)} %param.16, bf16[640,2048]{1,0:T(8,128)(2,1)} %all-gather.4.cloned.1.call-done, f32[2048]{0:T(1024)S(1)} %copy-done.4, f32[640]{0:T(1024)S(1)} %get-tuple-element.14), kind=kOutput, calls=%fused_computation.38 | convolution fusion | flops 4702863360 | bytes 14559744 | tf_op jit(solution)/shard_map/dot_general | solution.py:109
  102.1 5.0 %fusion.17 = f32[640,1792]{1,0:T(8,128)S(1)} fusion(bf16[2048,1792]{1,0:T(8,128)(2,1)S(1)} %bitcast.78, bf16[640,2048]{1,0:T(8,128)(2,1)S(1)} %copy-done, f32[2048]{0:T(1024)S(1)} %copy-done.4, f32[640]{0:T(1024)S(1)} %get-tuple-element.14), kind=kOutput, calls=%fused_computation.39 | convolution fusion | flops 4702863360 | bytes 14559744 | tf_op jit(solution)/shard_map/dot_general | solution.py:108
  107.2 5.0 %fusion.6 = f32[640,2048]{1,0:T(8,128)S(1)} fusion(bf16[1792,2048]{1,0:T(8,128)(2,1)S(1)} %bitcast.76, f32[640,1792]{1,0:T(8,128)S(1)} %fusion.15, f32[640,1792]{1,0:T(8,128)S(1)} %fusion.17), kind=kOutput, calls=%fused_computation.20 | convolution fusion | flops 4704501760 | bytes 21757952 | tf_op jit(solution)/shard_map/dot_general | solution.py:112
  112.2 1.6 multiply_reduce_fusion
  114.0 19.5 %reduce-scatter.3.cloned.1.call-done = bf16[20,512]{1,0:T(8,128)(2,1)} async-done(((bf16[20,2048]{1,0:T(8,128)(2,1)}), bf16[20,512]{1,0:T(8,128)(2,1)}) %reduce-scatter.3.cloned.1.call-update) | async-done | bytes 20496 | tf_op jit(solution)/shard_map/reduce_scatter | solution.py:117
  135.1 5.5 %all-to-all-start.3 = ((bf16[8,4,512]{2,1,0:T(4,128)(2,1)}), bf16[8,4,512]{2,1,0:T(4,128)(2,1)S(1)}, u32[]{:S(2)}, u32[]{:S(2)}) async-start(bf16[8,4,512]{2,1,0:T(4,128)(2,1)} %convert_element_type.244), calls=%async_computation.4 | async-start | bytes 65536 | tf_op jit(solution)/shard_map/all_to_all | solution.py:126
  141.7 5.6 %all-to-all-done.3 = bf16[8,4,512]{2,1,0:T(4,128)(2,1)S(1)} async-done(((bf16[8,4,512]{2,1,0:T(4,128)(2,1)}), bf16[8,4,512]{2,1,0:T(4,128)(2,1)S(1)}, u32[]{:S(2)}, u32[]{:S(2)}) %all-to-all-start.3) | async-done | bytes 32800 | tf_op jit(solution)/shard_map/all_to_all | solution.py:126
  147.6 30.6 %all_gather.20 = bf16[64,512]{1,0:T(8,128)(2,1)S(1)} all-gather(bf16[8,512]{1,0:T(8,128)(2,1)S(1)} %divide_convert_fusion.1), channel_id=1, replica_groups=mesh['dp'=8,'mp'=4] {'dp'}, dimensions={0}, use_global_device_ids=true | all-gather | bytes 73728 | tf_op jit(solution)/shard_map/all_gather | solution.py:142
  178.4 10.4 %all-reduce.2 = (bf16[128,64]{0,1:T(8,128)(2,1)S(1)}, bf16[64]{0:T(256)(128)(2,1)S(1)}, bf16[128]{0:T(256)(128)(2,1)S(1)}) all-reduce(bf16[128,64]{0,1:T(8,128)(2,1)S(1)} %fusion.14, bf16[64]{0:T(256)(128)(2,1)S(1)} %multiply_reduce_fusion.2, bf16[128]{0:T(256)(128)(2,1)S(1)} %multiply_reduce_fusion.1), channel_id=1, replica_groups=mesh['dp'=8,'mp'=4] {'mp'}, use_global_device_ids=true, to_apply=%region_11.12 | all-reduce | flops 8384 | bytes 33536 | tf_op jit(solution)/shard_map/psum | solution.py:151
  190.0 17.8 %all-reduce.1 = bf16[64]{0:T(256)(128)(2,1)S(1)} all-reduce(bf16[64]{0:T(256)(128)(2,1)S(1)} %fusion.24), channel_id=5, replica_groups=mesh['dp'=8,'mp'=4] {'dp'}, use_global_device_ids=true, to_apply=%region_21.22.clone | all-reduce | flops 64 | bytes 256
  207.9 41.0 %reduce-scatter.5.cloned.1.call-done = bf16[8,512]{1,0:T(8,128)(2,1)} async-done(((bf16[64,512]{1,0:T(8,128)(2,1)}), bf16[8,512]{1,0:T(8,128)(2,1)}) %reduce-scatter.5.cloned.1.call-update) | async-done | bytes 8208 | tf_op jit(solution)/shard_map/reduce_scatter | solution.py:185
  250.5 3.6 all-to-all-start.4
  254.2 6.6 %all-to-all-done.4 = bf16[8,4,512]{2,1,0:T(4,128)(2,1)S(1)} async-done(((bf16[8,4,512]{2,1,0:T(4,128)(2,1)}), bf16[8,4,512]{2,1,0:T(4,128)(2,1)S(1)}, u32[]{:S(2)}, u32[]{:S(2)}) %all-to-all-start.4) | async-done | bytes 32800 | tf_op jit(solution)/shard_map/all_to_all | solution.py:202
  260.9 5.3 %all_gather.21 = bf16[20,2048]{1,0:T(8,128)(2,1)S(1)} all-gather(bf16[20,512]{1,0:T(8,128)(2,1)S(1)} %get-tuple-element.22), channel_id=1, replica_groups=mesh['dp'=8,'mp'=4] {'mp'}, dimensions={1}, use_global_device_ids=true | all-gather | bytes 102400 | tf_op jit(solution)/shard_map/all_gather | solution.py:212
  266.6 9.9 %fusion.72 = f32[640,1792]{1,0:T(8,128)} fusion(bf16[640,2048]{1,0:T(8,128)(2,1)S(1)} %fusion.5, bf16[1792,2048]{1,0:T(8,128)(2,1)} %param.17), kind=kOutput, calls=%fused_computation.149 | convolution fusion | flops 4697620480 | bytes 14548992 | tf_op jit(solution)/shard_map/dot_general | solution.py:20
  276.5 14.3 %fusion.9 = f32[640,2048]{1,0:T(8,128)} fusion(bf16[2048,1792]{1,0:T(8,128)(2,1)S(1)} %bitcast.80, f32[640,1792]{1,0:T(8,128)} %copy-done.8, f32[640,1792]{1,0:T(8,128)} %fusion.72, f32[640,1792]{1,0:T(8,128)} %copy-done.9), kind=kOutput, calls=%fused_computation.23 | convolution fusion | flops 4709089280 | bytes 26345472 | tf_op jit(solution)/shard_map/dot_general | solution.py:20
  290.8 13.7 %add_convert_fusion = bf16[640,2048]{1,0:T(8,128)(2,1)} fusion(f32[640,2048]{1,0:T(8,128)} %fusion.9, bf16[2048,1792]{1,0:T(8,128)(2,1)} %param.16, f32[640,1792]{1,0:T(8,128)} %fusion.72, f32[640,1792]{1,0:T(8,128)} %copy-done.8), kind=kOutput, calls=%fused_computation.14 | convolution fusion | flops 4707123200 | bytes 24379392 | tf_op jit(solution)/shard_map/dot_general | solution.py:20
  304.7 67.6 %all-gather.6.cloned.1.call-done = bf16[2560,2048]{1,0:T(8,128)(2,1)} async-done(((bf16[640,2048]{1,0:T(8,128)(2,1)}), bf16[2560,2048]{1,0:T(8,128)(2,1)}) %all-gather.6.cloned.1.call-update) | async-done | bytes 10485776 | tf_op jit(solution)/shard_map/all_gather | solution.py:15
  372.3 7.3 %reduce_sum.151 = bf16[640,2048]{1,0:T(8,128)(2,1)S(1)} reduce(bf16[4,640,2048]{2,1,0:T(8,128)(2,1)} %bitcast.60, bf16[]{:T(256)} %constant.112.clone.1), dimensions={0}, to_apply=%region_22.23 | reduce | flops 3932160 | bytes 13107202 | tf_op jit(solution)/shard_map/reduce_sum | solution.py:16
  385.0 5.5 %all-to-all-start.5 = ((bf16[8,4,16384]{2,1,0:T(4,128)(2,1)}), bf16[8,4,16384]{2,1,0:T(4,128)(2,1)S(1)}, u32[]{:S(2)}, u32[]{:S(2)}) async-start(bf16[8,4,16384]{2,1,0:T(4,128)(2,1)} %reshape.491), calls=%async_computation.7 | async-start | bytes 2097152 | tf_op jit(solution)/shard_map/all_to_all | solution.py:240
  391.0 25.7 %all-to-all-done.5 = bf16[8,4,16384]{2,1,0:T(4,128)(2,1)S(1)} async-done(((bf16[8,4,16384]{2,1,0:T(4,128)(2,1)}), bf16[8,4,16384]{2,1,0:T(4,128)(2,1)S(1)}, u32[]{:S(2)}, u32[]{:S(2)}) %all-to-all-start.5) | async-done | bytes 1048608 | tf_op jit(solution)/shard_map/all_to_all | solution.py:240
  (138 shorter events, 25.6 us)
Async XLA Ops:
  26.8 9.8 %all-to-all-start = ((bf16[8,1,4]{2,1,0:T(2,128)(2,1)}), bf16[8,1,4]{2,1,0:T(2,128)(2,1)S(1)}, u32[]{:S(2)}, u32[]{:S(2)}) async-start(bf16[8,1,4]{2,1,0:T(2,128)(2,1)} %copy.53), calls=%async_computation | async-start | bytes 8192 | tf_op jit(solution)/shard_map/all_to_all | solution.py:93
  36.6 28.3 %copy-start.5 = (s32[1024]{0:T(1024)S(1)}, s32[1024]{0:T(1024)}, u32[]{:S(2)}) copy-start(s32[1024]{0:T(1024)} %param.10) | copy-start | bytes 12292
  36.6 32.9 %copy-start.7 = (s32[2]{0:T(128)S(1)}, s32[2]{0:T(128)}, u32[]{:S(2)}) copy-start(s32[2]{0:T(128)} %param.11) | copy-start | bytes 28
  36.6 33.5 %copy-start.6 = (s32[128]{0:T(128)S(1)}, s32[128]{0:T(128)}, u32[]{:S(2)}) copy-start(s32[128]{0:T(128)} %param.12) | copy-start | bytes 1540
  36.6 25.9 %all-to-all-start.1 = ((bf16[8,4,32,512]{3,2,1,0:T(8,128)(2,1)}), bf16[8,4,32,512]{3,2,1,0:T(8,128)(2,1)S(1)}, u32[]{:S(2)}, u32[]{:S(2)}) async-start(bf16[8,4,32,512]{3,2,1,0:T(8,128)(2,1)} %bitcast.18), calls=%async_computation.1 | async-start | bytes 2097152 | tf_op jit(solution)/shard_map/all_to_all | solution.py:91
  40.3 49.1 %all-gather.4.cloned.1.call-start = ((), (), s32[]{:S(2)}) async-start(), calls=%async_computation.8 | async-start | bytes 3276800 | tf_op jit(solution)/shard_map/all_gather | solution.py:104
  63.6 28.4 %copy-start.4 = (f32[2048]{0:T(1024)S(1)}, f32[2048]{0:T(1024)}, u32[]{:S(2)}) copy-start(f32[2048]{0:T(1024)} %param.14) | copy-start | bytes 24580
  65.8 9.9 %all-to-all-start.2 = ((bf16[8,4,32]{2,1,0:T(4,128)(2,1)}), bf16[8,4,32]{2,1,0:T(4,128)(2,1)S(1)}, u32[]{:S(2)}, u32[]{:S(2)}) async-start(bf16[8,4,32]{2,1,0:T(4,128)(2,1)} %bitcast.4), calls=%async_computation.2 | async-start | bytes 16384 | tf_op jit(solution)/shard_map/all_to_all | solution.py:92
  69.2 64.3 %reduce-scatter.3.cloned.1.call-start = ((), (), s32[]{:S(2)}) async-start(), calls=%async_computation.9 | async-start | bytes 122880 | tf_op jit(solution)/shard_map/reduce_scatter | solution.py:117
  89.4 12.7 %slice-start.2 = ((s8[7340032]{0:T(1024)(128)(4,1)}), s8[4194304]{0:T(1024)(128)(4,1)S(1)}, s32[]{:S(2)}) async-start(s8[7340032]{0:T(1024)(128)(4,1)} %bitcast.77), calls=%async_computation.14 | async-start | bytes 8388608
  89.4 17.7 %slice-start = ((s8[7340032]{0:T(1024)(128)(4,1)}), s8[4194304]{0:T(1024)(128)(4,1)S(1)}, s32[]{:S(2)}) async-start(s8[7340032]{0:T(1024)(128)(4,1)} %bitcast.75), calls=%async_computation.12 | async-start | bytes 8388608
  91.9 10.2 %copy-start = (bf16[640,2048]{1,0:T(8,128)(2,1)S(1)}, bf16[640,2048]{1,0:T(8,128)(2,1)}, u32[]{:S(2)}) copy-start(bf16[640,2048]{1,0:T(8,128)(2,1)} %all-gather.4.cloned.1.call-done) | copy-start | bytes 7864324
  91.9 10.2 %slice-start.3 = ((s8[7340032]{0:T(1024)(128)(4,1)}), s8[3145728]{0:T(1024)(128)(4,1)S(1)}, s32[]{:S(2)}) async-start(s8[7340032]{0:T(1024)(128)(4,1)} %bitcast.77), calls=%async_computation.15 | async-start | bytes 6291456
  91.9 15.2 %slice-start.1 = ((s8[7340032]{0:T(1024)(128)(4,1)}), s8[3145728]{0:T(1024)(128)(4,1)S(1)}, s32[]{:S(2)}) async-start(s8[7340032]{0:T(1024)(128)(4,1)} %bitcast.75), calls=%async_computation.13 | async-start | bytes 6291456
  102.1 5.0 %copy-start.9 = (f32[640,1792]{1,0:T(8,128)}, f32[640,1792]{1,0:T(8,128)S(1)}, u32[]{:S(2)}) copy-start(f32[640,1792]{1,0:T(8,128)S(1)} %fusion.15) | copy-start | bytes 13762564
  107.1 5.0 %copy-start.8 = (f32[640,1792]{1,0:T(8,128)}, f32[640,1792]{1,0:T(8,128)S(1)}, u32[]{:S(2)}) copy-start(f32[640,1792]{1,0:T(8,128)S(1)} %fusion.17) | copy-start | bytes 13762564
  112.2 28.5 %copy-start.3 = (bf16[128,512]{1,0:T(8,128)(2,1)S(1)}, bf16[128,512]{1,0:T(8,128)(2,1)}, u32[]{:S(2)}) copy-start(bf16[128,512]{1,0:T(8,128)(2,1)} %param.13) | copy-start | bytes 393220
  135.1 12.2 %all-to-all-start.3 = ((bf16[8,4,512]{2,1,0:T(4,128)(2,1)}), bf16[8,4,512]{2,1,0:T(4,128)(2,1)S(1)}, u32[]{:S(2)}, u32[]{:S(2)}) async-start(bf16[8,4,512]{2,1,0:T(4,128)(2,1)} %convert_element_type.244), calls=%async_computation.4 | async-start | bytes 65536 | tf_op jit(solution)/shard_map/all_to_all | solution.py:126
  140.6 108.3 %reduce-scatter.5.cloned.1.call-start = ((), (), s32[]{:S(2)}) async-start(), calls=%async_computation.10 | async-start | bytes 73728 | tf_op jit(solution)/shard_map/reduce_scatter | solution.py:185
  250.5 10.3 %all-to-all-start.4 = ((bf16[8,4,512]{2,1,0:T(4,128)(2,1)}), bf16[8,4,512]{2,1,0:T(4,128)(2,1)S(1)}, u32[]{:S(2)}, u32[]{:S(2)}) async-start(bf16[8,4,512]{2,1,0:T(4,128)(2,1)} %reshape.488), calls=%async_computation.6 | async-start | bytes 65536 | tf_op jit(solution)/shard_map/all_to_all | solution.py:202
  254.1 118.2 %all-gather.6.cloned.1.call-start = ((), (), s32[]{:S(2)}) async-start(), calls=%async_computation.11 | async-start | bytes 13107200 | tf_op jit(solution)/shard_map/all_gather | solution.py:15
  266.3 10.2 %slice-start.4 = ((s8[7340032]{0:T(1024)(128)(4,1)}), s8[4194304]{0:T(1024)(128)(4,1)S(1)}, s32[]{:S(2)}) async-start(s8[7340032]{0:T(1024)(128)(4,1)} %bitcast.79), calls=%async_computation.16 | async-start | bytes 8388608
  266.6 9.9 %slice-start.5 = ((s8[7340032]{0:T(1024)(128)(4,1)}), s8[3145728]{0:T(1024)(128)(4,1)S(1)}, s32[]{:S(2)}) async-start(s8[7340032]{0:T(1024)(128)(4,1)} %bitcast.79), calls=%async_computation.17 | async-start | bytes 6291456
  379.6 1.7 copy-start.1
  381.3 1.1 copy-start.2
  385.0 31.7 %all-to-all-start.5 = ((bf16[8,4,16384]{2,1,0:T(4,128)(2,1)}), bf16[8,4,16384]{2,1,0:T(4,128)(2,1)S(1)}, u32[]{:S(2)}, u32[]{:S(2)}) async-start(bf16[8,4,16384]{2,1,0:T(4,128)(2,1)} %reshape.491), calls=%async_computation.7 | async-start | bytes 2097152 | tf_op jit(solution)/shard_map/all_to_all | solution.py:240
Sparse Core Ops, SparseCore 0:
  65.0 24.3 all-gather.3
  113.9 19.5 reduce-scatter.2
  190.0 58.8 reduce-scatter.4
  304.7 67.5 all-gather.5
